TPU v7x, 32 devices: a whole 2x2x4 slice. The times are simulated.
32 devices in a mesh: prow: 4 (over y, x), pcol: 8 (over z, core).
Axes of the slice: x: 2, y: 2, z: 4, core: 2. Of those that a mesh axis runs over, the one named last changes fastest.
Arguments:
- inverse_factor: float32 [1024, 1024], P('pcol'), as said below
- diag_block: float32 [1024, 1024], P('pcol'), as said below
- panel_matrix: float32 [16, 4, 128, 1024], P(None, 'prow', 'pcol'), may hold values from -6 to 6
- panel_factor: float32 [16, 4, 128, 1024], P(None, 'prow', 'pcol'), may hold values from -0.1875 to 0.1875
- trailing: float32 [16, 4, 128, 8, 8, 128], P(None, 'prow', None, None, 'pcol'), may hold values from -6 to 6
Outputs:
- reduced_diag: float32 [1024, 1024], P('pcol')
- panel_result: float32 [16, 4, 128, 1024], P(None, 'prow', 'pcol')
- trailing_out: float32 [16, 4, 128, 8, 8, 128], P(None, 'prow', None, None, 'pcol')
Inputs may be any that keep to these rules, and one draw needn't show every extreme that they name: `inverse_factor`: lower triangular, diagonal entries between 0.5 and 2. `diag_block`: symmetric.
All inputs are finite; a program needn't handle non-finite values.
Results may differ from a plain program's by a relative error of at most 0.0003.
Values sent between devices are 32-bit elements; how exact they have to be, the bound alone decides.
No kernel may reach another device: no remote copies, remote signals or barrier semaphores. Data moves between devices by JAX's collectives and lax.ppermute only.
A program may use at most 128 MiB of HBM per device.

v0:
```python
import jax
import jax.numpy as jnp
from jax import lax
from jax.sharding import PartitionSpec as P


def broadcast(array, axis, root):
    mine = lax.axis_index(axis) == root
    return lax.psum(jnp.where(mine, array, jnp.zeros_like(array)), axis)


def body(inverse_factor, diag_block, panel_matrix, panel_factor, trailing):
    exact = lax.Precision.HIGHEST
    grid_rows = lax.axis_size("prow")
    grid_cols = lax.axis_size("pcol")
    column = lax.axis_index("pcol")
    grid_row = lax.axis_index("prow")
    local_rows = inverse_factor.shape[0]
    width = inverse_factor.shape[1]
    inverse_full = lax.all_gather(inverse_factor, "pcol", axis=0, tiled=True)
    diag_terms = jnp.dot(
        diag_block, inverse_full.T, precision=exact, preferred_element_type=jnp.float32
    )
    terms_full = lax.all_gather(diag_terms, "pcol", axis=0, tiled=True)
    reduced = jnp.dot(inverse_full, terms_full, precision=exact, preferred_element_type=jnp.float32)
    reduced_rows = lax.dynamic_slice_in_dim(reduced, column * local_rows, local_rows, 0)
    shape = panel_matrix.shape
    solved = jnp.dot(
        panel_matrix.reshape(-1, width),
        inverse_full.T,
        precision=exact,
        preferred_element_type=jnp.float32,
    )
    coupled = jnp.dot(
        panel_factor.reshape(-1, width),
        reduced,
        precision=exact,
        preferred_element_type=jnp.float32,
    )
    shifted = solved - 0.5 * coupled
    panel_result = (shifted - 0.5 * coupled).reshape(shape)
    rows_y, rows_l = (
        lax.all_gather(shifted.reshape(shape), "pcol", axis=2, tiled=True),
        lax.all_gather(panel_factor, "pcol", axis=2, tiled=True),
    )
    tile_rows = rows_y.shape[0]
    tile = rows_y.shape[2]
    col_tiles = trailing.shape[3]
    stride = grid_cols // grid_rows
    picked = column // grid_rows

    def select(rows):
        grouped = rows.reshape(col_tiles, stride, tile, width)
        return lax.dynamic_index_in_dim(grouped, picked, 1, keepdims=False)

    col_y, col_l = (
        broadcast(select(rows_y), "prow", column % grid_rows),
        broadcast(select(rows_l), "prow", column % grid_rows),
    )
    rows_y = rows_y.reshape(tile_rows, tile, width)
    rows_l = rows_l.reshape(tile_rows, tile, width)
    block = trailing.reshape(tile_rows, tile, col_tiles, tile)
    row_ids = jnp.arange(tile_rows, dtype=jnp.int32) * grid_rows + grid_row
    col_ids = jnp.arange(col_tiles, dtype=jnp.int32) * grid_cols + column
    lower = (row_ids[:, None] >= col_ids[None, :])[:, None, :, None]
    update = jnp.einsum(
        "isk,jtk->isjt", rows_y, col_l, precision=exact, preferred_element_type=jnp.float32
    )
    update = update + jnp.einsum(
        "isk,jtk->isjt", rows_l, col_y, precision=exact, preferred_element_type=jnp.float32
    )
    result = jnp.where(lower, block - update, block)
    return (reduced_rows, panel_result, result.reshape(trailing.shape))


def solution(mesh):
    in_specs = (
        P("pcol", None),
        P("pcol", None),
        P(None, "prow", "pcol", None),
        P(None, "prow", "pcol", None),
        P(None, "prow", None, None, "pcol", None),
    )
    out_specs = (
        P("pcol", None),
        P(None, "prow", "pcol", None),
        P(None, "prow", None, None, "pcol", None),
    )
    return jax.shard_map(body, mesh=mesh, in_specs=in_specs, out_specs=out_specs, check_vma=False)
```

profile of v0, /device:TPU:0, one launch (start us, length us, event | category | flops | bytes accessed | tf_op | source)
XLA Modules:
  0.0 531.9 jit_solution(17164543631338080142)
XLA Ops:
  7.2 0.0 copy-start
  7.2 0.0 all-gather.5.cloned.1.call-start
  7.2 0.7 all-gather.5.cloned.1.call-update
  7.9 0.0 all-gather.7.cloned.1.call-start
  8.0 51.2 %all-gather.5.cloned.1.call-done = f32[1024,1024]{1,0:T(8,128)} async-done(((f32[128,1024]{1,0:T(8,128)}), f32[1024,1024]{1,0:T(8,128)}) %all-gather.5.cloned.1.call-update) | async-done | bytes 4194320 | tf_op jit(solution)/shard_map/all_gather | solution.py:20
  59.2 7.5 %fusion.15 = f32[128,1024]{1,0:T(8,128)} fusion(f32[128,1024]{1,0:T(8,128)} %param.6, f32[1024,1024]{1,0:T(8,128)} %all-gather.5.cloned.1.call-done), kind=kOutput, calls=%fused_computation.21 | convolution fusion | flops 1610612736 | bytes 5242880 | tf_op jit(solution)/shard_map/dot_general | solution.py:21
  66.7 0.0 all-gather.7.cloned.1.call-update
  66.8 0.0 all-gather.11.cloned.1.call-start
  66.8 0.7 all-gather.11.cloned.1.call-update
  67.5 0.0 copy-start.5
  67.5 0.0 all-gather.9.cloned.1.call-start
  67.6 45.0 %all-gather.7.cloned.1.call-done = f32[1024,1024]{1,0:T(8,128)} async-done(((f32[128,1024]{1,0:T(8,128)}), f32[1024,1024]{1,0:T(8,128)}) %all-gather.7.cloned.1.call-update) | async-done | bytes 4194320 | tf_op jit(solution)/shard_map/all_gather | solution.py:24
  112.6 30.4 %fusion.16 = f32[1024,1024]{1,0:T(8,128)S(1)} fusion(f32[1024,1024]{1,0:T(8,128)} %all-gather.7.cloned.1.call-done, f32[1024,1024]{1,0:T(8,128)} %all-gather.5.cloned.1.call-done), kind=kOutput, calls=%fused_computation.22 | convolution fusion | flops 12884901888 | bytes 12582912 | tf_op jit(solution)/shard_map/dot_general | solution.py:25
  143.0 0.0 copy-start.3
  143.0 0.0 copy-start.2
  143.0 3.8 fusion.13
  146.9 5.1 fusion.14
  152.0 0.0 all-gather.9.cloned.1.call-update
  152.0 0.0 all-reduce.3.cloned.1.call-start
  152.1 43.0 %all-gather.11.cloned.1.call-done = f32[16,1,128,1024]{3,2,0,1:T(8,128)} async-done(((f32[16,1,16,1024]{3,2,0,1:T(8,128)}), f32[16,1,128,1024]{3,2,0,1:T(8,128)}) %all-gather.11.cloned.1.call-update) | async-done | bytes 8388624 | tf_op jit(solution)/shard_map/all_gather | solution.py:44
  195.1 5.0 fusion.6
  200.1 77.0 %all-gather.9.cloned.1.call-done = f32[16,1,128,1024]{3,2,0,1:T(8,128)} async-done(((f32[16,1,16,1024]{3,2,0,1:T(8,128)}), f32[16,1,128,1024]{3,2,0,1:T(8,128)}) %all-gather.9.cloned.1.call-update) | async-done | bytes 8388624 | tf_op jit(solution)/shard_map/all_gather | solution.py:43
  277.1 5.0 fusion.5
  282.0 0.0 all-reduce.3.cloned.1.call-update
  282.1 0.1 broadcast_compare_fusion
  282.2 1.1 dynamic-slice_bitcast_fusion
  283.3 1.0 copy.19
  284.3 168.5 %all-reduce.3.cloned.1.call-done = (f32[8,128,1024]{2,1,0:T(8,128)}, f32[8,128,1024]{2,1,0:T(8,128)}) async-done(((f32[8,128,1024]{2,1,0:T(8,128)}, f32[8,128,1024]{2,1,0:T(8,128)}), (f32[8,128,1024]{2,1,0:T(8,128)}, f32[8,128,1024]{2,1,0:T(8,128)})) %all-reduce.3.cloned.1.call-update) | async-done | bytes 8388624 | tf_op jit(solution)/shard_map/psum | solution.py:9
  452.8 30.9 %fusion.3 = f32[16,128,8,128]{3,1,2,0:T(8,128)S(1)} fusion(f32[16,1,128,1024]{3,2,0,1:T(8,128)} %all-gather.9.cloned.1.call-done, f32[8,128,1024]{2,1,0:T(8,128)} %get-tuple-element.9), kind=kOutput, calls=%fused_computation.4 | convolution fusion | flops 25769803776 | bytes 20971520 | tf_op jit(solution)/shard_map/isk,jtk->isjt/dot_general | solution.py:66
  483.7 31.5 %fusion = f32[16,1,128,8,1,128]{5,2,3,0,4,1:T(8,128)S(1)} fusion(f32[16,128,8,128]{3,1,2,0:T(8,128)S(1)} %fusion.3, f32[16,1,128,8,1,128]{5,4,3,2,1,0:T(1,128)} %param.9, pred[16,8]{1,0:T(8,128)(4,1)S(1)} %broadcast_compare_fusion, f32[16,1,128,1024]{3,2,0,1:T(8,128)} %all-gather.11.cloned.1.call-done, f32[8,128,1024]{2,1,0:T(8,128)S(1)} %copy-done.4), kind=kOutput, calls=%fused_computation.1 | convolution fusion | flops 25776095232 | bytes 37748864 | tf_op jit(solution)/shard_map/isk,jtk->isjt/dot_general | solution.py:69
  515.2 0.0 copy-start.1
  515.2 9.8 %copy.21 = f32[16,1,128,8,1,128]{5,4,3,2,1,0:T(1,128)} copy(f32[16,1,128,8,1,128]{5,2,3,0,4,1:T(8,128)S(1)} %fusion) | data formatting | bytes 16777216
  (9 shorter events, 0.0 us)
Async XLA Ops:
  7.2 139.7 %copy-start = (f32[16,1,16,1024]{3,2,1,0:T(8,128)S(1)}, f32[16,1,16,1024]{3,2,1,0:T(8,128)}, u32[]{:S(2)}) copy-start(f32[16,1,16,1024]{3,2,1,0:T(8,128)} %param.7) | copy-start | bytes 3145732
  7.2 52.0 %all-gather.5.cloned.1.call-start = ((), (), s32[]{:S(2)}) async-start(), calls=%async_computation | async-start | bytes 4718592 | tf_op jit(solution)/shard_map/all_gather | solution.py:20
  7.9 104.7 %all-gather.7.cloned.1.call-start = ((), (), s32[]{:S(2)}) async-start(), calls=%async_computation.1 | async-start | bytes 4718592 | tf_op jit(solution)/shard_map/all_gather | solution.py:24
  66.8 128.3 %all-gather.11.cloned.1.call-start = ((), (), s32[]{:S(2)}) async-start(), calls=%async_computation.3 | async-start | bytes 9437184 | tf_op jit(solution)/shard_map/all_gather | solution.py:44
  67.5 75.5 %copy-start.5 = (f32[16,1,16,1024]{3,2,1,0:T(8,128)S(1)}, f32[16,1,16,1024]{3,2,1,0:T(8,128)}, u32[]{:S(2)}) copy-start(f32[16,1,16,1024]{3,2,1,0:T(8,128)} %param.8) | copy-start | bytes 3145732
  67.5 209.6 %all-gather.9.cloned.1.call-start = ((), (), s32[]{:S(2)}) async-start(), calls=%async_computation.2 | async-start | bytes 9437184 | tf_op jit(solution)/shard_map/all_gather | solution.py:43
  143.0 9.0 %copy-start.3 = (f32[1024,1024]{1,0:T(8,128)}, f32[1024,1024]{1,0:T(8,128)S(1)}, u32[]{:S(2)}) copy-start(f32[1024,1024]{1,0:T(8,128)S(1)} %fusion.16) | copy-start | bytes 12582916
  143.0 3.9 copy-start.2
  152.0 300.8 %all-reduce.3.cloned.1.call-start = ((), (), s32[]{:S(2)}) async-start(), calls=%async_computation.4 | async-start | bytes 16777216 | tf_op jit(solution)/shard_map/psum | solution.py:9
  452.8 30.9 %copy-start.4 = (f32[8,128,1024]{2,1,0:T(8,128)S(1)}, f32[8,128,1024]{2,1,0:T(8,128)}, u32[]{:S(2)}) copy-start(f32[8,128,1024]{2,1,0:T(8,128)} %get-tuple-element.10) | copy-start | bytes 12582916
  515.2 9.8 %copy-start.1 = (f32[16,1,16,1024]{3,2,1,0:T(8,128)S(1)}, f32[16,1,16,1024]{3,2,1,0:T(8,128)}, u32[]{:S(2)}) copy-start(f32[16,1,16,1024]{3,2,1,0:T(8,128)} %param.7) | copy-start | bytes 3145732
Sparse Core Ops, SparseCore 0:
  9.6 49.5 all-gather.4
  66.9 45.6 all-gather.6
  114.2 80.8 all-gather.10
  196.5 80.5 all-gather.8
  282.2 170.5 all-reduce.2
where the time goes:
time: 535 us; the launch traced here: 532 us
  waiting for transfers between devices  386 us (72%)
  matrix products  109 us (20%)
  between operations  14.2 us (3%)
  local copies, waits for them, and re-layouts  11.9 us (2%)
  other arithmetic  10 us (2%)
    psum x1, waiting for transfers between devices, broadcast(): return lax.psum(jnp.where(mine, array, jnp.zeros_like(array)), axis)  169 us
    all_gather x1, waiting for transfers between devices, body(): lax.all_gather(shifted.reshape(shape), 'pcol', axis=2, tiled=True)  77 us
    all_gather x1, waiting for transfers between devices, body(): inverse_full = lax.all_gather(inverse_factor, 'pcol', axis=0, tiled=True)  51.2 us
    all_gather x1, waiting for transfers between devices, body(): terms_full = lax.all_gather(diag_terms, 'pcol', axis=0, tiled=True)  45 us
    all_gather x1, waiting for transfers between devices, body(): lax.all_gather(panel_factor, 'pcol', axis=2, tiled=True)  43 us
    dot_general x1, matrix products, body(): jnp.einsum('isk,jtk->isjt', rows_l, col_y, precision=exact, preferred_ele...  31.5 us
    dot_general x1, matrix products, body(): jnp.einsum('isk,jtk->isjt', rows_y, col_l, precision=exact, preferred_ele...  30.9 us
    dot_general x1, matrix products, body(): jnp.dot(inverse_full, terms_full, precision=exact, preferred_element_type...  30.4 us
  transfers between devices with their start and end apart: 5, of which 5 were waited for; matrix products, arithmetic and copies ran while one was open for 9% of the time, Pallas kernels for 0%

commit v1 on v0

--- a/solution.py
+++ b/solution.py
@@ -1,7 +1,353 @@
+import functools
+
 import jax
 import jax.numpy as jnp
 from jax import lax
+from jax.experimental import pallas as pl
+from jax.experimental.pallas import tpu as pltpu
 from jax.sharding import PartitionSpec as P
+
+
+F32 = jnp.float32
+BF16 = jnp.bfloat16
+EXTRA = 8
+
+
+def split(x):
+    high = x.astype(BF16)
+    return high, (x - high.astype(F32)).astype(BF16)
+
+
+def dot(a, b):
+    return jnp.dot(a, b, preferred_element_type=F32)
+
+
+def dot3(a, b_high, b_low):
+    high, low = split(a)
+    return dot(high, b_high) + (dot(low, b_high) + dot(high, b_low))
+
+
+def dot_nt(a, b):
+    return lax.dot_general(a, b, (((1,), (1,)), ((), ())), preferred_element_type=F32)
+
+
+def call(kernel, outs, ins, scalars, scratch=(), grid=None, in_specs=None, out_specs=None, alias=None, flops=0):
+    whole = pl.BlockSpec(memory_space=pltpu.VMEM)
+    spec = pltpu.PrefetchScalarGridSpec(
+        num_scalar_prefetch=1,
+        grid=grid or (1,),
+        in_specs=in_specs or [whole] * len(ins),
+        out_specs=out_specs or [whole] * len(outs),
+        scratch_shapes=list(scratch),
+    )
+    moved = sum(a.size * a.dtype.itemsize for a in (*ins, *outs))
+    return pl.pallas_call(
+        kernel,
+        out_shape=outs,
+        grid_spec=spec,
+        input_output_aliases=alias or {},
+        cost_estimate=pl.CostEstimate(flops=flops, bytes_accessed=moved, transcendentals=0),
+        compiler_params=pltpu.CompilerParams(vmem_limit_bytes=50 * 2**20),
+    )(jnp.stack([jnp.asarray(s, jnp.int32) for s in scalars]), *ins)
+
+
+def unpack_kernel(s, rows, cols, extra, inv_h, inv_l, tr_h, tr_l, a_h, a_l):
+    step = pl.program_id(0)
+    size, width = rows.shape
+    row = step * size + lax.broadcasted_iota(jnp.int32, (size, width), 0)
+    col = lax.broadcasted_iota(jnp.int32, (size, width), 1)
+    mine = rows[...]
+    inv_h[...], inv_l[...] = split(jnp.where(row >= col, mine, 0.0))
+    flipped = cols[...].T
+    tr_h[...], tr_l[...] = split(jnp.where(col >= row, flipped, 0.0))
+    diag = jnp.broadcast_to(extra[0, 0:1, 0:size], (size, size))
+    spread = jnp.concatenate([diag] * (width // size), axis=1)
+    a = jnp.where(col > row, mine, jnp.where(col < row, flipped, spread))
+    a_h[...], a_l[...] = split(a)
+
+
+def unpack(packed, extra):
+    width = packed.shape[0]
+    size = width // extra.shape[0]
+    out = jax.ShapeDtypeStruct((width, width), BF16)
+    row = pl.BlockSpec((size, width), lambda i, s: (i, 0))
+    return call(
+        unpack_kernel,
+        [out] * 6,
+        (packed, packed, extra),
+        (0,),
+        grid=(width // size,),
+        in_specs=[row, pl.BlockSpec((width, size), lambda i, s: (0, i)), pl.BlockSpec((1, *extra.shape[1:]), lambda i, s: (i, 0, 0))],
+        out_specs=[row] * 6,
+        flops=10**9,
+    )
+
+
+def place_kernel(s, ref, out, extra):
+    size = out.shape[0]
+    out[...] = ref[0, 0, 0, 0:size, :]
+    extra[...] = ref[0, 0, 0, size : size + EXTRA, :][None]
+
+
+def place(stacked, line, core, grid_row, size):
+    _, rows, length, _, part = stacked.shape
+    shard = lambda i, s: 2 * ((i // rows) % length ^ s[0]) + (i // (rows * length) ^ s[1])
+    out = jax.ShapeDtypeStruct((2 * length * size, rows * part), F32)
+    extra = jax.ShapeDtypeStruct((2 * length, EXTRA, rows * part), F32)
+    return call(
+        place_kernel,
+        [out, extra],
+        (stacked,),
+        (line, core, grid_row),
+        grid=(2 * length * rows,),
+        in_specs=[pl.BlockSpec((1, 1, 1, size + EXTRA, part), lambda i, s: (i // (rows * length), i % rows, (i // rows) % length, 0, 0))],
+        out_specs=[
+            pl.BlockSpec((size, part), lambda i, s: (shard(i, s), i % rows ^ s[2])),
+            pl.BlockSpec((1, EXTRA, part), lambda i, s: (shard(i, s), 0, i % rows ^ s[2])),
+        ],
+        flops=10**8,
+    )
+
+
+def pair_of(panel, factor, mats):
+    inv_h, inv_l, tr_h, tr_l, a_h, a_l = mats
+    g = dot3(factor, inv_h[...], inv_l[...])
+    rest = panel - dot3(g, a_h[...], a_l[...])
+    return g, rest, (tr_h[...], tr_l[...])
+
+
+def own_kernel(s, panel, factor, inv, *refs):
+    *mats, reduced, result = refs
+    width = panel.shape[-1]
+    _, rest, flipped = pair_of(panel[...].reshape(-1, width), factor[...].reshape(-1, width), mats)
+    result[...] = dot3(rest, *flipped).reshape(result.shape)
+    reduced[...] = dot3(dot3(inv[...], mats[4][...], mats[5][...]), *flipped)
+
+
+def column_kernel(carried, s, kept, got, *refs):
+    mats, (out_h, out_l) = refs[:6], refs[6 + carried :]
+    tiles, depth, wide = kept.shape[1:]
+    first = s[1] == 0
+    a, b = kept[...].reshape(-1, wide), got[...].reshape(-1, wide)
+    g, rest, flipped = pair_of(jnp.where(first, a, b), jnp.where(first, b, a), mats)
+    h = dot3(rest, *flipped)
+    for at, value in ((0, g), (wide, h)):
+        for piece, out in zip(split(value), (out_h, out_l), strict=True):
+            for k in range(2):
+                for j in range(tiles):
+                    from_row = (k * tiles + j) * depth
+                    out[j, k * depth : (k + 1) * depth, at : at + wide] = piece[from_row : from_row + depth]
+
+
+def column(kept, got, mats, buffers, position, core, tile):
+    _, tiles, depth, width = kept.shape
+    whole = lambda a: pl.BlockSpec(a.shape, lambda i, s: (0,) * a.ndim)
+    block = pl.BlockSpec((tiles, 2 * depth, 2 * width), lambda i, s: (0, s[0], 0))
+    out = jax.ShapeDtypeStruct((tiles, tile, 2 * width), BF16)
+    ins = (kept, got, *mats, *buffers)
+    fixed = len(ins) - len(buffers)
+    return call(
+        functools.partial(column_kernel, len(buffers)),
+        [out, out],
+        ins,
+        (position, core),
+        in_specs=[whole(a) for a in ins[:fixed]] + [pl.BlockSpec(memory_space=pl.ANY)] * len(buffers),
+        out_specs=[block, block],
+        alias={fixed + 1 + n: n for n in range(len(buffers))},
+        flops=18 * kept.size * width,
+    )
+
+
+def trailing_kernel(count, rows, s, *refs):
+    units = refs[: 4 * count]
+    g_h, g_l, _, out, lhs_h, lhs_l, acc, buf, sem = refs[4 * count :]
+    step = pl.program_id(0)
+    wanted, core, lead = s[count], s[count + 1], s[count + 2]
+    tiles, depth, wide = units[0].shape[1:]
+    group = 4 * depth
+    per = count * group
+    lines = 2 * depth * tiles
+
+    def at(slot):
+        start = pl.multiple_of(s[slot] * lines, lines)
+        return out.at[:, pl.ds(start, lines), :]
+
+    @pl.when(step == 0)
+    def _():
+        for slot in range(count):
+            pltpu.make_async_copy(at(slot), buf.at[slot], sem.at[slot]).start()
+        for slot in range(count):
+            for unit in range(4):
+                ref = units[4 * slot + unit]
+                q = wanted if unit < 2 else 1 - wanted
+                k = core if unit % 2 == 0 else 1 - core
+                offset = pl.multiple_of(slot * group + q * 2 * depth + k * depth, depth)
+                for half in range(2):
+                    for j in range(tiles):
+                        high, low = split(ref[half, j])
+                        lhs_h[j, pl.ds(offset, depth), half * wide : (half + 1) * wide] = high
+                        lhs_l[j, pl.ds(offset, depth), half * wide : (half + 1) * wide] = low
+        for slot in range(count):
+            pltpu.make_async_copy(at(slot), buf.at[slot], sem.at[slot]).wait()
+
+    part = 256
+    tile = g_h.shape[1]
+
+    def block(n):
+        height = (tiles - 2 * n) * per
+
+        def one(i, first):
+            here = pl.ds(pl.multiple_of(i * part, part), part)
+            x_h = lhs_h[2 * n :, :, here].reshape(height, part)
+            x_l = lhs_l[2 * n :, :, here].reshape(height, part)
+            r_h = g_h[:, :, here].reshape(2 * tile, part)
+            r_l = g_l[:, :, here].reshape(2 * tile, part)
+            value = dot_nt(x_h, r_h) + dot_nt(x_l, r_h) + dot_nt(x_h, r_l)
+            acc[0:height] = value if first else acc[0:height] + value
+
+        one(0, True)
+        lax.fori_loop(1, 2 * wide // part, lambda i, c: (one(i, False), c)[1], 0)
+        for j in range(2 * n, tiles):
+            for slot in range(count):
+                for q in range(2):
+                    base = (j - 2 * n) * per + slot * group + q * 2 * depth
+                    for which in range(2):
+                        column_tile = 2 * n + which
+                        if column_tile > j:
+                            continue
+                        value = acc[base : base + 2 * depth, which * tile : (which + 1) * tile]
+                        if column_tile == j:
+                            value = jnp.where(rows * q + lead >= 0, value, 0.0)
+                        there = pl.ds(column_tile, 2 * depth, stride=tiles)
+                        buf[slot, 2 * j + q, there, :] = buf[slot, 2 * j + q, there, :] - value
+
+    for n in range(tiles // 2):
+        pl.when(step == n)(functools.partial(block, n))
+
+    @pl.when(step == tiles // 2 - 1)
+    def _():
+        for slot in range(count):
+            pltpu.make_async_copy(buf.at[slot], at(slot), sem.at[slot]).start()
+        for slot in range(count):
+            pltpu.make_async_copy(buf.at[slot], at(slot), sem.at[slot]).wait()
+
+
+def update(slots, positions, wanted, core, lead, rows, high, low, state):
+    units = [u for slot in slots for u in slot]
+    count = len(slots)
+    tiles, depth, wide = units[0].shape[1:]
+    tile = high.shape[1]
+    whole = pl.BlockSpec(units[0].shape, lambda i, s: (0, 0, 0, 0))
+    right = pl.BlockSpec((2, tile, 2 * wide), lambda i, s: (i, 0, 0))
+    any_space = pl.BlockSpec(memory_space=pl.ANY)
+    ins = (*units, high, low, state)
+    per = count * 4 * depth
+    lhs = pltpu.VMEM((tiles, per, 2 * wide), BF16)
+    return call(
+        functools.partial(trailing_kernel, count, rows),
+        [jax.ShapeDtypeStruct(state.shape, F32)],
+        ins,
+        (*positions, wanted, core, lead),
+        scratch=[
+            lhs,
+            lhs,
+            pltpu.VMEM((tiles * per, 2 * tile), F32),
+            pltpu.VMEM((count, 2 * tiles, 2 * depth * tiles, tile), F32),
+            pltpu.SemaphoreType.DMA((count,)),
+        ],
+        grid=(tiles // 2,),
+        in_specs=[whole] * len(units) + [right, right, any_space],
+        out_specs=[any_space],
+        alias={len(ins): 0},
+        flops=6 * tiles * per * 2 * wide * tiles * tile,
+    )[0]
+
+
+def permute(a, axis, pairs):
+    return lax.ppermute(a, axis, pairs)
+
+
+def fast_body(inverse_factor, diag_block, panel_matrix, panel_factor, trailing):
+    rows, cols = lax.axis_size("prow"), lax.axis_size("pcol")
+    length = cols // 2
+    p, g = lax.axis_index("pcol"), lax.axis_index("prow")
+    line, core = p // 2, p % 2
+    size, width = inverse_factor.shape
+    tile_rows, _, depth, _ = panel_matrix.shape
+    tiles, tile = trailing.shape[3], trailing.shape[2]
+    sel = jnp.where
+    low_side = line < length // 2
+    end = (line == 0) | (line == length - 1)
+    wanted = p // rows
+
+    outer = [(a, a ^ 2) for a in range(cols)]
+    inner = [(2 * l + k, 2 * o + k) for a in range(1, length - 1, 2) for k in range(2) for l, o in ((a, a + 1), (a + 1, a))]
+    A = lambda a: permute(a, "pcol", outer)
+    B = lambda a: permute(a, "pcol", inner)
+    D = lambda a: permute(a, "pcol", [(b, b ^ 1) for b in range(cols)])
+    Y = lambda a: permute(a, "prow", [(b, b ^ 2) for b in range(rows)])
+    X = lambda a: permute(a, "prow", [(b, b ^ 1) for b in range(rows)])
+
+    row = p * size + lax.broadcasted_iota(jnp.int32, (size, width), 0)
+    col = lax.broadcasted_iota(jnp.int32, (size, width), 1)
+    diag = jnp.sum(sel(row == col, diag_block, 0.0), axis=1)
+    mixed = sel(row >= col, inverse_factor, diag_block)
+    part = width // rows
+    quarter = lax.dynamic_slice_in_dim(mixed, g * part, part, 1)
+    head = jnp.pad(diag[None], ((0, EXTRA - 1), (0, part - size)))
+    quarter = jnp.concatenate([quarter, head])
+    gathered = jnp.stack([quarter] + [permute(quarter, "pcol", [(a, a ^ (2 * k)) for a in range(cols)]) for k in range(1, length)])
+
+    both = jnp.stack([panel_matrix, panel_factor]).reshape(2, tiles, 2, depth, width)
+    want = sel(low_side, both[:, :, 0], both[:, :, 1])
+    other = sel(low_side, both[:, :, 1], both[:, :, 0])
+
+    a1f = A(sel(end, other, want))
+    b1f = B(other)
+    a2f = A(sel(end, want, b1f))
+    b2f = B(a1f)
+    a3f = A(b2f)
+    a1s = A(other)
+    b1s = B(want)
+    a2s = A(b1s)
+    b2s = B(a2f)
+    a3s = A(b2s)
+    first = [want, sel(end, a1f, b1f), sel(end, a2f, b2f), sel(end, a3f, a2f)]
+    second = [other, sel(end, a1s, b1s), sel(end, a2s, b2s), sel(end, a3s, a1f)]
+    first_swapped = [D(a) for a in first]
+    second_swapped = [D(a) for a in second]
+    slots = list(zip(first, first_swapped, second, second_swapped, strict=True))
+    positions = [sel(low_side, line + n, line - n + length) % length for n in range(length)]
+
+    m_two = jnp.stack([gathered, Y(gathered)])
+    m_four = jnp.stack([m_two, X(m_two)], axis=1)
+    m_all = jnp.stack([m_four, D(m_four)])
+    packed, extra = place(m_all.reshape(2, rows, length, size + EXTRA, part), line, core, g, size)
+    mats = unpack(packed, extra)
+
+    def spread(own, swapped):
+        mine = sel(core == 0, jnp.stack([own[0], swapped[0]]), jnp.stack([swapped[1], own[1]]))
+        held = sel(g // 2 == line % 2, mine, Y(mine))
+        across = X(held)
+        send_across = (g % 2 == 0) == (core == 0)
+        return sel(send_across, held, across), D(sel(send_across, across, held))
+
+    buffers = ()
+    for n in range(length):
+        kept, got = spread(first[n], first_swapped[n])
+        buffers = column(kept, got, mats, buffers, positions[n], core, tile)
+
+    reduced, result = call(
+        own_kernel,
+        [jax.ShapeDtypeStruct((size, width), F32), jax.ShapeDtypeStruct((tile_rows, depth, width), F32)],
+        (panel_matrix.reshape(tile_rows, depth, width), panel_factor.reshape(tile_rows, depth, width), inverse_factor, *mats),
+        (0,),
+        flops=18 * panel_matrix.size * width + 12 * size * width * width,
+    )
+    state = trailing.reshape(tile_rows, tile * tiles, tile)
+    for some in (slice(0, 2), slice(2, 4)):
+        state = update(slots[some], positions[some], wanted, core, g - p, rows, *buffers, state)
+    return reduced, result.reshape(panel_matrix.shape), state.reshape(trailing.shape)
 
 
 def broadcast(array, axis, root):
@@ -9,7 +355,7 @@
     return lax.psum(jnp.where(mine, array, jnp.zeros_like(array)), axis)
 
 
-def body(inverse_factor, diag_block, panel_matrix, panel_factor, trailing):
+def plain_body(inverse_factor, diag_block, panel_matrix, panel_factor, trailing):
     exact = lax.Precision.HIGHEST
     grid_rows = lax.axis_size("prow")
     grid_cols = lax.axis_size("pcol")
@@ -74,6 +420,7 @@
 
 
 def solution(mesh):
+    rows, cols = mesh.shape["prow"], mesh.shape["pcol"]
     in_specs = (
         P("pcol", None),
         P("pcol", None),
@@ -86,4 +433,9 @@
         P(None, "prow", "pcol", None),
         P(None, "prow", None, None, "pcol", None),
     )
+    fast = rows == 4 and cols == 2 * rows
+
+    def body(*args):
+        return (fast_body if fast else plain_body)(*args)
+
     return jax.shard_map(body, mesh=mesh, in_specs=in_specs, out_specs=out_specs, check_vma=False)

time: 535 us -> 368 us (0.69)
  waiting for transfers between devices: 386 us -> 109 us
  Pallas kernels: 0 us -> 138 us
  matrix products: 109 us -> 0 us
  starting transfers between devices: 0.2 us -> 72.2 us
  other arithmetic: 10 us -> 28.9 us
  between operations: 14.2 us -> 1.45 us
    all_gather x4 -> x0, waiting for transfers between devices: 216 us -> none  [the longest x1 77 us: body(): lax.all_gather(shifted.reshape(shape), 'pcol', axis=2, tiled=True)]
    psum x1 -> x0, waiting for transfers between devices: 169 us -> none  [broadcast(): return lax.psum(jnp.where(mine, array, jnp.zeros_like(array)), axis)]
    pallas_call x0 -> x9, Pallas kernels: none -> 138 us  [call(): pl.pallas_call(kernel, out_shape=outs, grid_spec=spec, input_output_alias...]
    dot_general x6 -> x0, matrix products: 109 us -> none  [the longest x1 31.5 us: body(): jnp.einsum('isk,jtk->isjt', rows_l, col_y, precision=exact, preferred_ele...]
    ppermute x0 -> x36, waiting for transfers between devices: none -> 109 us  [permute(): return lax.ppermute(a, axis, pairs)]
    ppermute x0 -> x36, starting transfers between devices: none -> 72.2 us  [permute(): return lax.ppermute(a, axis, pairs)]
    select_n x2 -> x19, other arithmetic: 9.94 us -> 21.5 us  [the longest x4 6.82 us: spread(): return (sel(send_across, held, across), D(sel(send_across, across, held)))]
    another operation x0 -> x10, other arithmetic: none -> 7.21 us  [the longest x1 2.5 us: fast_body(): m_all = jnp.stack([m_four, D(m_four)])]
  transfers between devices with their start and end apart: 5 -> 36, of which waited for: 5 -> 9; matrix products, arithmetic and copies ran while one was open for 9% -> 8% of each run, Pallas kernels for 0% -> 32%
where the time goes in v1:
time: 368 us; the launch traced here: 361 us
  Pallas kernels  138 us (38%)
  waiting for transfers between devices  109 us (30%)
  starting transfers between devices  72.2 us (20%)
  other arithmetic  28.9 us (8%)
  local copies, waits for them, and re-layouts  11.5 us (3%)
    pallas_call x9, Pallas kernels, call(): pl.pallas_call(kernel, out_shape=outs, grid_spec=spec, input_output_alias...  138 us
    ppermute x36, waiting for transfers between devices, permute(): return lax.ppermute(a, axis, pairs)  109 us
    ppermute x36, starting transfers between devices, permute(): return lax.ppermute(a, axis, pairs)  72.2 us
    unnamed x51, local copies, waits for them, and re-layouts  10.3 us
  transfers between devices with their start and end apart: 36, of which 9 were waited for; matrix products, arithmetic and copies ran while one was open for 8% of the time, Pallas kernels for 32%

profile of v1, /device:TPU:0, one launch (start us, length us, event | category | flops | bytes accessed | tf_op | source)
XLA Modules:
  0.0 360.9 jit_solution(5189563659730492900)
XLA Ops:
  0.7 7.8 %copy.44 = f32[16,1,128,8,1,128]{5,4,3,2,1,0:T(1,128)} copy(f32[16,1,128,8,1,128]{5,4,3,2,1,0:T(1,128)} %param.9) | data formatting | bytes 16777216
  10.4 5.1 %collective-permute-start.2 = (f32[136,256]{1,0:T(8,128)}, f32[136,256]{1,0:T(8,128)S(1)}, u32[]{:S(2)}, u32[]{:S(2)}) collective-permute-start(f32[136,256]{1,0:T(8,128)} %get-tuple-element.81), channel_id=1, source_target_pairs={{0,6},{1,7},{2,4},{3,5},{4,2},{5,3},{6,0},{7,1},{8,14},{9,15},{10,... | collective-permute-start | bytes 417800 | tf_op jit(solution)/shard_map/ppermute | solution.py:267
  16.0 1.8 broadcast_select_fusion.18
  19.3 1.6 collective-permute-start.6
  21.0 7.5 %collective-permute-done.1 = f32[136,256]{1,0:T(8,128)} collective-permute-done((f32[136,256]{1,0:T(8,128)}, f32[136,256]{1,0:T(8,128)}, u32[]{:S(2)}, u32[]{:S(2)}) %collective-permute-start.1) | collective-permute-done | bytes 139296 | tf_op jit(solution)/shard_map/ppermute | solution.py:267
  28.5 2.1 fusion.4
  32.1 1.7 collective-permute-start.11
  34.3 9.4 %collective-permute-done.3 = f32[4,136,256]{2,1,0:T(8,128)} collective-permute-done((f32[4,136,256]{2,1,0:T(8,128)}, f32[4,136,256]{2,1,0:T(8,128)}, u32[]{:S(2)}, u32[]{:S(2)}) %collective-permute-start.3) | collective-permute-done | bytes 557088 | tf_op jit(solution)/shard_map/ppermute | solution.py:267
  48.7 1.8 broadcast_select_fusion.13
  50.7 23.3 %collective-permute-start.34 = (f32[2,8,16,1024]{3,2,1,0:T(8,128)}, f32[2,8,16,1024]{3,2,1,0:T(8,128)S(1)}, u32[]{:S(2)}, u32[]{:S(2)}) collective-permute-start(f32[2,8,16,1024]{3,2,1,0:T(8,128)} %get-tuple-element.47.refs_2_), channel_id=1, source_target_pairs={{0,2},{1,3},{2,0},{3,1},{4,6},{5,7},{6,4},{7,5},{8,10},{9,11},{10,... | collective-permute-start | bytes 3145736 | tf_op jit(solution)/shard_map/ppermute | solution.py:267
  74.3 1.6 collective-permute-start.30
  76.0 19.4 %collective-permute-start.15 = (f32[2,8,16,1024]{3,2,1,0:T(8,128)S(1)}, f32[2,8,16,1024]{3,2,1,0:T(8,128)S(1)}, u32[]{:S(2)}, u32[]{:S(2)}) collective-permute-start(f32[2,8,16,1024]{3,2,1,0:T(8,128)S(1)} %collective-permute-done.9), channel_id=1, source_target_pairs={{0,2},{1,3},{2,0},{3,1},{4,6},{5,7},{6,4},{7,5},{8,10},{9,11},{10,... | collective-permute-start | bytes 3145736 | tf_op jit(solution)/shard_map/ppermute | solution.py:267
  95.9 2.4 collective-permute-done.34
  98.4 22.3 %collective-permute-done.7 = f32[2,8,16,1024]{3,2,1,0:T(8,128)S(1)} collective-permute-done((f32[2,8,16,1024]{3,2,1,0:T(8,128)S(1)}, f32[2,8,16,1024]{3,2,1,0:T(8,128)S(1)}, u32[]{:S(2)}, u32[]{:S(2)}) %collective-permute-start.7) | collective-permute-done | bytes 1048608 | tf_op jit(solution)/shard_map/ppermute | solution.py:267
  124.6 18.6 %collective-permute-done.15 = f32[2,8,16,1024]{3,2,1,0:T(8,128)S(1)} collective-permute-done((f32[2,8,16,1024]{3,2,1,0:T(8,128)S(1)}, f32[2,8,16,1024]{3,2,1,0:T(8,128)S(1)}, u32[]{:S(2)}, u32[]{:S(2)}) %collective-permute-start.15) | collective-permute-done | bytes 1048608 | tf_op jit(solution)/shard_map/ppermute | solution.py:267
  145.0 18.2 %collective-permute-done.12 = f32[2,8,16,1024]{3,2,1,0:T(8,128)S(1)} collective-permute-done((f32[2,8,16,1024]{3,2,1,0:T(8,128)}, f32[2,8,16,1024]{3,2,1,0:T(8,128)S(1)}, u32[]{:S(2)}, u32[]{:S(2)}) %collective-permute-start.12) | collective-permute-done | bytes 1048608 | tf_op jit(solution)/shard_map/ppermute | solution.py:267
  173.6 2.5 pad_maximum_fusion.ref
  176.1 18.7 %shard_map.76 = (f32[1024,1024]{1,0:T(8,128)}, f32[8,8,1024]{2,1,0:T(8,128)S(1)}) custom-call(s32[3]{0:T(128)S(1)} %pad_add_fusion.s, f32[2,4,4,136,256]{4,3,2,1,0:T(8,128)} %pad_maximum_fusion.ref), custom_call_target="tpu_custom_call" | custom-call | flops 100000000 | bytes 8912896 | tf_op jit(solution)/shard_map/pallas_call | solution.py:44
  194.8 10.9 %shard_map.77 = (bf16[1024,1024]{1,0:T(8,128)(2,1)S(1)}, bf16[1024,1024]{1,0:T(8,128)(2,1)}, bf16[1024,1024]{1,0:T(8,128)(2,1)}, bf16[1024,1024]{1,0:T(8,128)(2,...) custom-call(s32[1]{0:T(128)} %constant.102.clone.1.s, f32[1024,1024]{1,0:T(8,128)} %get-tuple-element.21.rows.cols, ...), custom_call_target="tpu_custom_call" | custom-call | flops 1000000000 | bytes 21233664 | tf_op jit(solution)/shard_map/pallas_call | solution.py:44
  207.1 12.4 %shard_map.78 = (f32[128,1024]{1,0:T(8,128)}, f32[16,16,1024]{2,1,0:T(8,128)}) custom-call(s32[1]{0:T(128)} %constant.102.clone.1.s, f32[16,16,1024]{2,1,0:T(8,128)S(1)} %bitcast.67, f32[16,16,1024]{2,1,0:T(8,128)S(1)} %bitcast.69, f32[128,1024]{1,0:T(8,128)S(1)} %copy-done.4, bf16[1024,1024]{1,0:T(8,128)(2,1)} %copy-done, ...), custom_call_target="tpu_custom_call" | custom-call | flops 6442450944 | bytes 16777216 | tf_op jit(solution)/shard_map/pallas_call | solution.py:44
  219.5 1.8 collective-permute-start.17
  225.1 1.8 broadcast_select_fusion.6
  226.9 11.8 %shard_map.79 = (bf16[8,128,2048]{2,1,0:T(8,128)(2,1)}, bf16[8,128,2048]{2,1,0:T(8,128)(2,1)}) custom-call(s32[2]{0:T(128)S(1)} %pad_add_fusion.4.s, f32[2,8,16,1024]{3,2,1,0:T(8,128)S(1)} %get-tuple-element.49.kept, f32[2,8,16,1024]{3,2,1,0:T(8,128)S(1)} %collective-permute-done.32.got, bf16[1024,1024]{1,0:T(8,128)(2,1)} %copy-done, ...), custom_call_target="tpu_custom_call" | custom-call | flops 4831838208 | bytes 23068672 | tf_op jit(solution)/shard_map/pallas_call | solution.py:44
  238.7 10.2 %collective-permute-done.23 = f32[2,8,16,1024]{3,2,1,0:T(8,128)S(1)} collective-permute-done((f32[2,8,16,1024]{3,2,1,0:T(8,128)}, f32[2,8,16,1024]{3,2,1,0:T(8,128)S(1)}, u32[]{:S(2)}, u32[]{:S(2)}) %collective-permute-start.23) | collective-permute-done | bytes 1048608 | tf_op jit(solution)/shard_map/ppermute | solution.py:267
  248.9 2.4 broadcast_select_fusion.8
  251.4 18.8 %collective-permute-done.20 = f32[2,8,16,1024]{3,2,1,0:T(8,128)} collective-permute-done((f32[2,8,16,1024]{3,2,1,0:T(8,128)S(1)}, f32[2,8,16,1024]{3,2,1,0:T(8,128)}, u32[]{:S(2)}, u32[]{:S(2)}) %collective-permute-start.20) | collective-permute-done | bytes 1048608 | tf_op jit(solution)/shard_map/ppermute | solution.py:267
  272.1 2.4 broadcast_select_fusion.14.refs_6_
  274.6 11.9 %shard_map.80 = (bf16[8,128,2048]{2,1,0:T(8,128)(2,1)}, bf16[8,128,2048]{2,1,0:T(8,128)(2,1)}) custom-call(s32[2]{0:T(128)S(1)} %pad_add_fusion.3.s, f32[2,8,16,1024]{3,2,1,0:T(8,128)S(1)} %get-tuple-element.51.kept, f32[2,8,16,1024]{3,2,1,0:T(8,128)S(1)} %collective-permute-done.28.got, ...), custom_call_target="tpu_custom_call", output_to_operand_aliasing={{0}: (9, {}), {1}: (10, {})} | custom-call | flops 4831838208 | bytes 31457280 | tf_op jit(solution)/shard_map/pallas_call | solution.py:44
  287.1 11.8 %shard_map.81 = (bf16[8,128,2048]{2,1,0:T(8,128)(2,1)}, bf16[8,128,2048]{2,1,0:T(8,128)(2,1)}) custom-call(s32[2]{0:T(128)S(1)} %pad_add_fusion.2.s, f32[2,8,16,1024]{3,2,1,0:T(8,128)S(1)} %get-tuple-element.53.kept, f32[2,8,16,1024]{3,2,1,0:T(8,128)S(1)} %collective-permute-done.24.got, ...), custom_call_target="tpu_custom_call", output_to_operand_aliasing={{0}: (9, {}), {1}: (10, {})} | custom-call | flops 4831838208 | bytes 31457280 | tf_op jit(solution)/shard_map/pallas_call | solution.py:44
  298.9 11.8 %shard_map.82 = (bf16[8,128,2048]{2,1,0:T(8,128)(2,1)}, bf16[8,128,2048]{2,1,0:T(8,128)(2,1)}) custom-call(s32[2]{0:T(128)S(1)} %pad_add_fusion.1.s, f32[2,8,16,1024]{3,2,1,0:T(8,128)S(1)} %get-tuple-element.55.kept, f32[2,8,16,1024]{3,2,1,0:T(8,128)S(1)} %collective-permute-done.21.got, ...), custom_call_target="tpu_custom_call", output_to_operand_aliasing={{0}: (9, {}), {1}: (10, {})} | custom-call | flops 4831838208 | bytes 31457280 | tf_op jit(solution)/shard_map/pallas_call | solution.py:44
  310.7 24.7 %shard_map.83.refs_10_ = f32[16,1024,128]{2,1,0:T(8,128)} custom-call(s32[5]{0:T(128)S(1)} %stack.175.s, f32[2,8,16,1024]{3,2,1,0:T(8,128)S(1)} %bitcast.65, f32[2,8,16,1024]{3,2,1,0:T(8,128)S(1)} %collective-permute-done.29.refs_1_, f32[2,8,16,1024]{3,2,1,0:T(8,128)} %get-tuple-element.47.refs_2_, ...), custom_call_target="tpu_custom_call", output_to_operand_aliasing={{}: (11, {})} | custom-call | flops 12884901888 | bytes 33554432 | tf_op jit(solution)/shard_map/pallas_call | solution.py:44
  336.5 24.2 %shard_map.84 = f32[16,1024,128]{2,1,0:T(8,128)} custom-call(s32[5]{0:T(128)S(1)} %stack.157.s, f32[2,8,16,1024]{3,2,1,0:T(8,128)S(1)} %get-tuple-element.77.refs_0_, f32[2,8,16,1024]{3,2,1,0:T(8,128)S(1)} %collective-permute-done.10.refs_1_, f32[2,8,16,1024]{3,2,1,0:T(8,128)S(1)} %broadcast_select_fusion.16.refs_2_, ...), custom_call_target="tpu_custom_call", output_to_operand_aliasing={{}: (11, {})} | custom-call | flops 12884901888 | bytes 33554432 | tf_op jit(solution)/shard_map/pallas_call | solution.py:44
  (142 shorter events, 36.7 us)
Async XLA Ops:
  15.5 13.1 %collective-permute-start.1 = (f32[136,256]{1,0:T(8,128)}, f32[136,256]{1,0:T(8,128)}, u32[]{:S(2)}, u32[]{:S(2)}) collective-permute-start(f32[136,256]{1,0:T(8,128)} %get-tuple-element.81), channel_id=1, source_target_pairs={{0,4},{1,5},{2,6},{3,7},{4,0},{5,1},{6,2},{7,3},{8,12},{9,13},{10,... | collective-permute-start | bytes 417800 | tf_op jit(solution)/shard_map/ppermute | solution.py:267
  15.5 13.1 %collective-permute-start = (f32[136,256]{1,0:T(8,128)}, f32[136,256]{1,0:T(8,128)}, u32[]{:S(2)}, u32[]{:S(2)}) collective-permute-start(f32[136,256]{1,0:T(8,128)} %get-tuple-element.81), channel_id=1, source_target_pairs={{0,2},{1,3},{2,0},{3,1},{4,6},{5,7},{6,4},{7,5},{8,10},{9,11},{10,... | collective-permute-start | bytes 417800 | tf_op jit(solution)/shard_map/ppermute | solution.py:267
  17.9 30.1 %collective-permute-start.8 = (f32[2,8,16,1024]{3,2,1,0:T(8,128)}, f32[2,8,16,1024]{3,2,1,0:T(8,128)}, u32[]{:S(2)}, u32[]{:S(2)}) collective-permute-start(f32[2,8,16,1024]{3,2,1,0:T(8,128)} %get-tuple-element.45), channel_id=1, source_target_pairs={{0,2},{1,3},{2,0},{3,1},{4,6},{5,7},{6,4},{7,5},{8,10},{9,11},{10,... | collective-permute-start | bytes 3145736 | tf_op jit(solution)/shard_map/ppermute | solution.py:267
  19.3 29.4 %collective-permute-start.6 = (f32[2,8,16,1024]{3,2,1,0:T(8,128)}, f32[2,8,16,1024]{3,2,1,0:T(8,128)}, u32[]{:S(2)}, u32[]{:S(2)}) collective-permute-start(f32[2,8,16,1024]{3,2,1,0:T(8,128)} %get-tuple-element.47.refs_2_), channel_id=1, source_target_pairs={{2,4},{4,2},{3,5},{5,3},{10,12},{12,10},{11,13},{13,11},{18,20},{2... | collective-permute-start | bytes 3145736 | tf_op jit(solution)/shard_map/ppermute | solution.py:267
  32.1 18.6 %collective-permute-start.11 = (f32[2,8,16,1024]{3,2,1,0:T(8,128)S(1)}, f32[2,8,16,1024]{3,2,1,0:T(8,128)}, u32[]{:S(2)}, u32[]{:S(2)}) collective-permute-start(f32[2,8,16,1024]{3,2,1,0:T(8,128)S(1)} %bitcast.63), channel_id=1, source_target_pairs={{2,4},{4,2},{3,5},{5,3},{10,12},{12,10},{11,13},{13,11},{18,20},{2... | collective-permute-start | bytes 3145736 | tf_op jit(solution)/shard_map/ppermute | solution.py:267
  33.8 40.2 %collective-permute-start.29 = (f32[2,8,16,1024]{3,2,1,0:T(8,128)S(1)}, f32[2,8,16,1024]{3,2,1,0:T(8,128)S(1)}, u32[]{:S(2)}, u32[]{:S(2)}) collective-permute-start(f32[2,8,16,1024]{3,2,1,0:T(8,128)S(1)} %bitcast.64), channel_id=1, source_target_pairs={{0,1},{1,0},{2,3},{3,2},{4,5},{5,4},{6,7},{7,6},{8,9},{9,8},{10,11... | collective-permute-start | bytes 3145736 | tf_op jit(solution)/shard_map/ppermute | solution.py:267
  45.1 29.3 %collective-permute-start.4 = (f32[2,4,136,256]{3,2,1,0:T(8,128)S(1)}, f32[2,4,136,256]{3,2,1,0:T(8,128)S(1)}, u32[]{:S(2)}, u32[]{:S(2)}) collective-permute-start(f32[2,4,136,256]{3,2,1,0:T(8,128)S(1)} %get-tuple-element.57), channel_id=1, source_target_pairs={{0,8},{8,0},{16,24},{24,16},{1,9},{9,1},{17,25},{25,17},{2,10},{10... | collective-permute-start | bytes 3342344 | tf_op jit(solution)/shard_map/ppermute | solution.py:267
  48.0 28.0 %collective-permute-start.9 = (f32[2,8,16,1024]{3,2,1,0:T(8,128)}, f32[2,8,16,1024]{3,2,1,0:T(8,128)S(1)}, u32[]{:S(2)}, u32[]{:S(2)}) collective-permute-start(f32[2,8,16,1024]{3,2,1,0:T(8,128)} %collective-permute-done.8), channel_id=1, source_target_pairs={{2,4},{4,2},{3,5},{5,3},{10,12},{12,10},{11,13},{13,11},{18,20},{2... | collective-permute-start | bytes 3145736 | tf_op jit(solution)/shard_map/ppermute | solution.py:267
  50.6 45.1 %collective-permute-start.25 = (f32[2,8,16,1024]{3,2,1,0:T(8,128)S(1)}, f32[2,8,16,1024]{3,2,1,0:T(8,128)S(1)}, u32[]{:S(2)}, u32[]{:S(2)}) collective-permute-start(f32[2,8,16,1024]{3,2,1,0:T(8,128)S(1)} %get-tuple-element.66.refs_4_), channel_id=1, source_target_pairs={{0,1},{1,0},{2,3},{3,2},{4,5},{5,4},{6,7},{7,6},{8,9},{9,8},{10,11... | collective-permute-start | bytes 3145736 | tf_op jit(solution)/shard_map/ppermute | solution.py:267
  50.7 47.5 %collective-permute-start.34 = (f32[2,8,16,1024]{3,2,1,0:T(8,128)}, f32[2,8,16,1024]{3,2,1,0:T(8,128)S(1)}, u32[]{:S(2)}, u32[]{:S(2)}) collective-permute-start(f32[2,8,16,1024]{3,2,1,0:T(8,128)} %get-tuple-element.47.refs_2_), channel_id=1, source_target_pairs={{0,2},{1,3},{2,0},{3,1},{4,6},{5,7},{6,4},{7,5},{8,10},{9,11},{10,... | collective-permute-start | bytes 3145736 | tf_op jit(solution)/shard_map/ppermute | solution.py:267
  74.1 46.7 %collective-permute-start.7 = (f32[2,8,16,1024]{3,2,1,0:T(8,128)S(1)}, f32[2,8,16,1024]{3,2,1,0:T(8,128)S(1)}, u32[]{:S(2)}, u32[]{:S(2)}) collective-permute-start(f32[2,8,16,1024]{3,2,1,0:T(8,128)S(1)} %get-tuple-element.67), channel_id=1, source_target_pairs={{0,2},{1,3},{2,0},{3,1},{4,6},{5,7},{6,4},{7,5},{8,10},{9,11},{10,... | collective-permute-start | bytes 3145736 | tf_op jit(solution)/shard_map/ppermute | solution.py:267
  74.3 49.3 %collective-permute-start.30 = (f32[2,8,16,1024]{3,2,1,0:T(8,128)S(1)}, f32[2,8,16,1024]{3,2,1,0:T(8,128)S(1)}, u32[]{:S(2)}, u32[]{:S(2)}) collective-permute-start(f32[2,8,16,1024]{3,2,1,0:T(8,128)S(1)} %maximum_select_fusion.3), channel_id=1, source_target_pairs={{0,16},{8,24},{16,0},{24,8},{1,17},{9,25},{17,1},{25,9},{2,18},{10... | collective-permute-start | bytes 3145736 | tf_op jit(solution)/shard_map/ppermute | solution.py:267
  76.0 67.2 %collective-permute-start.15 = (f32[2,8,16,1024]{3,2,1,0:T(8,128)S(1)}, f32[2,8,16,1024]{3,2,1,0:T(8,128)S(1)}, u32[]{:S(2)}, u32[]{:S(2)}) collective-permute-start(f32[2,8,16,1024]{3,2,1,0:T(8,128)S(1)} %collective-permute-done.9), channel_id=1, source_target_pairs={{0,2},{1,3},{2,0},{3,1},{4,6},{5,7},{6,4},{7,5},{8,10},{9,11},{10,... | collective-permute-start | bytes 3145736 | tf_op jit(solution)/shard_map/ppermute | solution.py:267
  95.7 67.5 %collective-permute-start.12 = (f32[2,8,16,1024]{3,2,1,0:T(8,128)}, f32[2,8,16,1024]{3,2,1,0:T(8,128)S(1)}, u32[]{:S(2)}, u32[]{:S(2)}) collective-permute-start(f32[2,8,16,1024]{3,2,1,0:T(8,128)} %collective-permute-done.11), channel_id=1, source_target_pairs={{0,2},{1,3},{2,0},{3,1},{4,6},{5,7},{6,4},{7,5},{8,10},{9,11},{10,... | collective-permute-start | bytes 3145736 | tf_op jit(solution)/shard_map/ppermute | solution.py:267
  98.3 70.3 %collective-permute-start.5 = (f32[2,2,4,136,256]{4,3,2,0,1:T(8,128)S(1)}, f32[2,2,4,136,256]{4,3,2,0,1:T(8,128)S(1)}, u32[]{:S(2)}, u32[]{:S(2)}) collective-permute-start(f32[2,2,4,136,256]{4,3,2,0,1:T(8,128)S(1)} %pad_maximum_fusion.1), channel_id=1, source_target_pairs={{0,1},{1,0},{2,3},{3,2},{4,5},{5,4},{6,7},{7,6},{8,9},{9,8},{10,11... | collective-permute-start | bytes 6684680 | tf_op jit(solution)/shard_map/ppermute | solution.py:267
  120.7 42.7 %collective-permute-start.26 = (f32[2,8,16,1024]{3,2,1,0:T(8,128)S(1)}, f32[2,8,16,1024]{3,2,1,0:T(8,128)S(1)}, u32[]{:S(2)}, u32[]{:S(2)}) collective-permute-start(f32[2,8,16,1024]{3,2,1,0:T(8,128)S(1)} %maximum_select_fusion.2), channel_id=1, source_target_pairs={{0,16},{8,24},{16,0},{24,8},{1,17},{9,25},{17,1},{25,9},{2,18},{10... | collective-permute-start | bytes 3145736 | tf_op jit(solution)/shard_map/ppermute | solution.py:267
  123.6 41.6 %collective-permute-start.13 = (f32[2,8,16,1024]{3,2,1,0:T(8,128)S(1)}, f32[2,8,16,1024]{3,2,1,0:T(8,128)S(1)}, u32[]{:S(2)}, u32[]{:S(2)}) collective-permute-start(f32[2,8,16,1024]{3,2,1,0:T(8,128)S(1)} %collective-permute-done.7), channel_id=1, source_target_pairs={{2,4},{4,2},{3,5},{5,3},{10,12},{12,10},{11,13},{13,11},{18,20},{2... | collective-permute-start | bytes 3145736 | tf_op jit(solution)/shard_map/ppermute | solution.py:267
  143.2 22.6 %collective-permute-start.31 = (f32[2,8,16,1024]{3,2,1,0:T(8,128)S(1)}, f32[2,8,16,1024]{3,2,1,0:T(8,128)S(1)}, u32[]{:S(2)}, u32[]{:S(2)}) collective-permute-start(f32[2,8,16,1024]{3,2,1,0:T(8,128)S(1)} %broadcast_select_fusion), channel_id=1, source_target_pairs={{0,8},{8,0},{16,24},{24,16},{1,9},{9,1},{17,25},{25,17},{2,10},{10... | collective-permute-start | bytes 3145736 | tf_op jit(solution)/shard_map/ppermute | solution.py:267
  165.2 145.5 %collective-permute-start.33 = (f32[2,8,16,1024]{3,2,1,0:T(8,128)}, f32[2,8,16,1024]{3,2,1,0:T(8,128)}, u32[]{:S(2)}, u32[]{:S(2)}) collective-permute-start(f32[2,8,16,1024]{3,2,1,0:T(8,128)} %get-tuple-element.47.refs_2_), channel_id=1, source_target_pairs={{0,1},{1,0},{2,3},{3,2},{4,5},{5,4},{6,7},{7,6},{8,9},{9,8},{10,11... | collective-permute-start | bytes 3145736 | tf_op jit(solution)/shard_map/ppermute | solution.py:267
  165.8 57.7 %collective-permute-start.27 = (f32[2,8,16,1024]{3,2,1,0:T(8,128)}, f32[2,8,16,1024]{3,2,1,0:T(8,128)}, u32[]{:S(2)}, u32[]{:S(2)}) collective-permute-start(f32[2,8,16,1024]{3,2,1,0:T(8,128)} %broadcast_select_fusion.1), channel_id=1, source_target_pairs={{0,8},{8,0},{16,24},{24,16},{1,9},{9,1},{17,25},{25,17},{2,10},{10... | collective-permute-start | bytes 3145736 | tf_op jit(solution)/shard_map/ppermute | solution.py:267
  168.6 58.3 %collective-permute-start.32 = (f32[2,8,16,1024]{3,2,1,0:T(8,128)}, f32[2,8,16,1024]{3,2,1,0:T(8,128)S(1)}, u32[]{:S(2)}, u32[]{:S(2)}) collective-permute-start(f32[2,8,16,1024]{3,2,1,0:T(8,128)} %get-tuple-element.48), channel_id=1, source_target_pairs={{0,1},{1,0},{2,3},{3,2},{4,5},{5,4},{6,7},{7,6},{8,9},{9,8},{10,11... | collective-permute-start | bytes 3145736 | tf_op jit(solution)/shard_map/ppermute | solution.py:267
  170.2 49.3 %collective-permute-start.22 = (f32[2,8,16,1024]{3,2,1,0:T(8,128)}, f32[2,8,16,1024]{3,2,1,0:T(8,128)}, u32[]{:S(2)}, u32[]{:S(2)}) collective-permute-start(f32[2,8,16,1024]{3,2,1,0:T(8,128)} %maximum_select_fusion.1), channel_id=1, source_target_pairs={{0,16},{8,24},{16,0},{24,8},{1,17},{9,25},{17,1},{25,9},{2,18},{10... | collective-permute-start | bytes 3145736 | tf_op jit(solution)/shard_map/ppermute | solution.py:267
  173.1 49.6 %collective-permute-start.19 = (f32[2,8,16,1024]{3,2,1,0:T(8,128)}, f32[2,8,16,1024]{3,2,1,0:T(8,128)}, u32[]{:S(2)}, u32[]{:S(2)}) collective-permute-start(f32[2,8,16,1024]{3,2,1,0:T(8,128)} %maximum_select_fusion), channel_id=1, source_target_pairs={{0,16},{8,24},{16,0},{24,8},{1,17},{9,25},{17,1},{25,9},{2,18},{10... | collective-permute-start | bytes 3145736 | tf_op jit(solution)/shard_map/ppermute | solution.py:267
  219.5 52.0 %collective-permute-start.17 = (f32[2,8,16,1024]{3,2,1,0:T(8,128)}, f32[2,8,16,1024]{3,2,1,0:T(8,128)}, u32[]{:S(2)}, u32[]{:S(2)}) collective-permute-start(f32[2,8,16,1024]{3,2,1,0:T(8,128)} %copy-done.21), channel_id=1, source_target_pairs={{0,2},{1,3},{2,0},{3,1},{4,6},{5,7},{6,4},{7,5},{8,10},{9,11},{10,... | collective-permute-start | bytes 3145736 | tf_op jit(solution)/shard_map/ppermute | solution.py:267
  222.7 26.2 %collective-permute-start.23 = (f32[2,8,16,1024]{3,2,1,0:T(8,128)}, f32[2,8,16,1024]{3,2,1,0:T(8,128)S(1)}, u32[]{:S(2)}, u32[]{:S(2)}) collective-permute-start(f32[2,8,16,1024]{3,2,1,0:T(8,128)} %broadcast_select_fusion.2), channel_id=1, source_target_pairs={{0,8},{8,0},{16,24},{24,16},{1,9},{9,1},{17,25},{25,17},{2,10},{10... | collective-permute-start | bytes 3145736 | tf_op jit(solution)/shard_map/ppermute | solution.py:267
  223.5 46.6 %collective-permute-start.20 = (f32[2,8,16,1024]{3,2,1,0:T(8,128)S(1)}, f32[2,8,16,1024]{3,2,1,0:T(8,128)}, u32[]{:S(2)}, u32[]{:S(2)}) collective-permute-start(f32[2,8,16,1024]{3,2,1,0:T(8,128)S(1)} %broadcast_select_fusion.3), channel_id=1, source_target_pairs={{0,8},{8,0},{16,24},{24,16},{1,9},{9,1},{17,25},{25,17},{2,10},{10... | collective-permute-start | bytes 3145736 | tf_op jit(solution)/shard_map/ppermute | solution.py:267
  226.9 47.7 %collective-permute-start.28 = (f32[2,8,16,1024]{3,2,1,0:T(8,128)S(1)}, f32[2,8,16,1024]{3,2,1,0:T(8,128)S(1)}, u32[]{:S(2)}, u32[]{:S(2)}) collective-permute-start(f32[2,8,16,1024]{3,2,1,0:T(8,128)S(1)} %get-tuple-element.50), channel_id=1, source_target_pairs={{0,1},{1,0},{2,3},{3,2},{4,5},{5,4},{6,7},{7,6},{8,9},{9,8},{10,11... | collective-permute-start | bytes 3145736 | tf_op jit(solution)/shard_map/ppermute | solution.py:267
  248.9 61.8 %collective-permute-start.35 = (f32[2,8,16,1024]{3,2,1,0:T(8,128)}, f32[2,8,16,1024]{3,2,1,0:T(8,128)}, u32[]{:S(2)}, u32[]{:S(2)}) collective-permute-start(f32[2,8,16,1024]{3,2,1,0:T(8,128)} %broadcast_select_fusion.12.refs_6_), channel_id=1, source_target_pairs={{0,1},{1,0},{2,3},{3,2},{4,5},{5,4},{6,7},{7,6},{8,9},{9,8},{10,11... | collective-permute-start | bytes 3145736 | tf_op jit(solution)/shard_map/ppermute | solution.py:267
  270.1 16.4 %collective-permute-start.24 = (f32[2,8,16,1024]{3,2,1,0:T(8,128)}, f32[2,8,16,1024]{3,2,1,0:T(8,128)S(1)}, u32[]{:S(2)}, u32[]{:S(2)}) collective-permute-start(f32[2,8,16,1024]{3,2,1,0:T(8,128)} %get-tuple-element.52), channel_id=1, source_target_pairs={{0,1},{1,0},{2,3},{3,2},{4,5},{5,4},{6,7},{7,6},{8,9},{9,8},{10,11... | collective-permute-start | bytes 3145736 | tf_op jit(solution)/shard_map/ppermute | solution.py:267
  271.6 27.3 %collective-permute-start.21 = (f32[2,8,16,1024]{3,2,1,0:T(8,128)S(1)}, f32[2,8,16,1024]{3,2,1,0:T(8,128)S(1)}, u32[]{:S(2)}, u32[]{:S(2)}) collective-permute-start(f32[2,8,16,1024]{3,2,1,0:T(8,128)S(1)} %get-tuple-element.54), channel_id=1, source_target_pairs={{0,1},{1,0},{2,3},{3,2},{4,5},{5,4},{6,7},{7,6},{8,9},{9,8},{10,11... | collective-permute-start | bytes 3145736 | tf_op jit(solution)/shard_map/ppermute | solution.py:267
  274.6 60.9 %collective-permute-start.14 = (f32[2,8,16,1024]{3,2,1,0:T(8,128)S(1)}, f32[2,8,16,1024]{3,2,1,0:T(8,128)}, u32[]{:S(2)}, u32[]{:S(2)}) collective-permute-start(f32[2,8,16,1024]{3,2,1,0:T(8,128)S(1)} %broadcast_select_fusion.16.refs_2_), channel_id=1, source_target_pairs={{0,1},{1,0},{2,3},{3,2},{4,5},{5,4},{6,7},{7,6},{8,9},{9,8},{10,11... | collective-permute-start | bytes 3145736 | tf_op jit(solution)/shard_map/ppermute | solution.py:267
  286.6 48.9 %collective-permute-start.18 = (f32[2,8,16,1024]{3,2,1,0:T(8,128)S(1)}, f32[2,8,16,1024]{3,2,1,0:T(8,128)S(1)}, u32[]{:S(2)}, u32[]{:S(2)}) collective-permute-start(f32[2,8,16,1024]{3,2,1,0:T(8,128)S(1)} %copy-done.22), channel_id=1, source_target_pairs={{0,1},{1,0},{2,3},{3,2},{4,5},{5,4},{6,7},{7,6},{8,9},{9,8},{10,11... | collective-permute-start | bytes 3145736 | tf_op jit(solution)/shard_map/ppermute | solution.py:267
  (29 other events, 266.3 us)
